TPU v7x, 512 devices: a 8x2x16 block of a 8x8x16 slice. The times are simulated.
512 devices in a mesh: groups: 2 (over y), users: 16 (over z), routers: 8 (over x), heads: 2 (over core).
Axes of the slice: x: 8, y: 2, z: 16, core: 2. Of those that a mesh axis runs over, the one named last changes fastest.
The devices are a block of a 8x8x16 slice.
Arguments:
- items: bfloat16 [4096, 64, 1024], P(('groups', 'users', 'routers')), parts along dimension 0, may hold values from -6 to 6
- block_owner: int32 [4096, 1], P(('groups', 'users', 'routers')), parts along dimension 0, may hold values from 0 to 15; in each aligned block of 16 rows (0 to 15, 16 to 31, ...) at most 2 rows name the same one
- block_user: int32 [4096], P(('groups', 'users', 'routers')), parts along dimension 0, may hold values from 0 to 1
- block_fill: int32 [4096], P(('groups', 'users', 'routers')), parts along dimension 0, may hold values from 1 to 64
- prefix_keys: bfloat16 [64, 256, 1024], P(('groups', 'users'), None, 'heads'), parts along dimension 0, may hold values from -6 to 6
- prefix_values: bfloat16 [64, 256, 1024], P(('groups', 'users'), None, 'heads'), parts along dimension 0, may hold values from -6 to 6
- w_in: bfloat16 [4, 1024, 1024], P(None, 'routers', 'heads'), may hold values from -0.1875 to 0.1875
- attn_gain: bfloat16 [1024], P('heads'), may hold values from 0.25 to 1.75
- w_o: bfloat16 [1024, 1024], P('heads', 'routers'), may hold values from -0.1875 to 0.1875
- mlp_gain: bfloat16 [1024], replicated, may hold values from 0.25 to 1.75
- w_one: bfloat16 [1024, 256], replicated, may hold values from -0.1875 to 0.1875
- w_two: bfloat16 [256], replicated, may hold values from -0.375 to 0.375
Outputs:
- scores: float32 [4096, 64], P(('groups', 'users', 'routers')), parts along dimension 0
There are 2 independent parts, one for each index of `groups`. A program takes and returns all parts, laid end to end along the dimension named above; an argument that names none is the same for every part. Nothing has to cross between parts.
Inputs may be any that keep to these rules, and one draw needn't show every extreme that they name: `block_owner`: within the rows of one device (aligned blocks of 16 blocks), no owner is named by more than 2 rows, and in every draw some owner is named by exactly 2 rows of some device.
All inputs are finite; a program needn't handle non-finite values.
Results may differ from a plain program's by a relative error of at most 0.005.
Values may be sent and summed in bfloat16 or wider, within the bound.
No kernel may reach another device: no remote copies, remote signals or barrier semaphores. Data moves between devices by JAX's collectives and lax.ppermute only.
A program may use at most 64 MiB of HBM per device.

v0:
```python
import jax
import jax.numpy as jnp
from jax import lax
from jax.sharding import PartitionSpec as P

D = 1024
HEAD_DIM = 128
CAP = 2
HD = 1024
EPSILON = 1e-05


def items_in_groups(x, axis, split_dim, concat_dim, work, item_dim, out_dim):

    def moved(group):
        return lax.all_to_all(group, axis, split_axis=split_dim, concat_axis=concat_dim, tiled=True)

    items = jax.tree.leaves(x)[0].shape[item_dim]
    ends = [items * k // 2 for k in range(2 + 1)] if items % 2 == 0 else [0, items]
    groups = [
        jax.tree.map(lambda a: lax.slice_in_dim(a, low, high, axis=item_dim), x)
        for low, high in zip(ends, ends[1:])
    ]
    arrived = [moved(group) for group in groups]
    made = [work(group) for group in arrived]
    return jax.tree.map(lambda *parts: jnp.concatenate(parts, axis=out_dim), *made)


def in_blocks(x, dim, peers):
    shape = x.shape
    tiles = x.reshape(*shape[:dim], peers, shape[dim] // peers, *shape[dim + 1 :])
    return jnp.moveaxis(tiles, dim, 0)


def sent_and_summed(x, axis, dim):
    tiles = in_blocks(x, dim, lax.axis_size(axis))
    arrived = lax.all_to_all(tiles, axis, split_axis=0, concat_axis=0, tiled=True)
    return arrived.sum(axis=0)


def sent_to_all(x, axis):
    copies = jnp.broadcast_to(x, (lax.axis_size(axis), *x.shape))
    return lax.all_to_all(copies, axis, split_axis=0, concat_axis=0, tiled=True)


def taken_together(x, axis):
    return sent_to_all(x, axis).sum(axis=0)


def prefix_attention(group_queries, group_users, prefix_keys, prefix_values):
    group_size, block_width, half_width = group_queries.shape
    heads_here = half_width // HEAD_DIM
    safe_user = jnp.maximum(group_users, 0)
    user_keys = jnp.take(prefix_keys, safe_user, axis=0)
    user_values = jnp.take(prefix_values, safe_user, axis=0)
    query_heads = group_queries.reshape(group_size, block_width, heads_here, HEAD_DIM)
    key_heads = user_keys.reshape(group_size, -1, heads_here, HEAD_DIM)
    value_heads = user_values.reshape(group_size, -1, heads_here, HEAD_DIM)
    raw_scores = jnp.einsum(
        "gqhd,gkhd->ghqk", query_heads, key_heads, preferred_element_type=jnp.float32
    ) * HEAD_DIM ** (-0.5)
    weights = jax.nn.silu(raw_scores).astype(jnp.bfloat16)
    summed = jnp.einsum("ghqk,gkhd->gqhd", weights, value_heads, preferred_element_type=jnp.float32)
    return summed.reshape(group_size, block_width, half_width).astype(jnp.bfloat16)


def local(
    items,
    block_owner,
    block_user,
    block_fill,
    prefix_keys,
    prefix_values,
    w_in,
    attn_gain,
    w_o,
    mlp_gain,
    w_one,
    w_two,
):
    blocks, block_width, model_width = items.shape
    row_count = blocks * block_width
    half_width = w_in.shape[2]
    heads_here = half_width // HEAD_DIM
    peer_count = lax.axis_size("users")
    slot_count = peer_count * CAP
    score_scale = HEAD_DIM ** (-0.5)
    flat_items = items.reshape(row_count, model_width)
    projected = jnp.einsum(
        "rk,pkc->prc",
        flat_items,
        lax.all_gather(w_in, "routers", axis=1, tiled=True),
        preferred_element_type=jnp.float32,
    )
    activated = jax.nn.silu(projected)
    queries = activated[0].astype(jnp.bfloat16)
    target = block_owner[:, 0]
    earlier = lax.broadcasted_iota(jnp.int32, (blocks, blocks), 1) < lax.broadcasted_iota(
        jnp.int32, (blocks, blocks), 0
    )
    same_target = target[:, None] == target[None, :]
    dest_rank = jnp.sum((same_target & earlier).astype(jnp.int32), axis=1)
    position = target * CAP + dest_rank
    selector = lax.broadcasted_iota(jnp.int32, (slot_count, blocks), 0) == position[None, :]
    block_queries = queries.reshape(blocks, block_width * half_width)
    outgoing = jnp.dot(
        selector.astype(jnp.bfloat16), block_queries, preferred_element_type=jnp.float32
    ).astype(jnp.bfloat16)
    outgoing = outgoing.reshape(peer_count, CAP, block_width, half_width)
    slot_user = jnp.sum(jnp.where(selector, block_user[None, :] + 1, 0), axis=1) - 1
    slot_user = slot_user.reshape(peer_count, CAP)

    def serve_slots(received):
        arrived, arrived_users = received
        sources, per_source = arrived_users.shape
        total_slots = sources * per_source
        flat_queries = arrived.reshape(total_slots, block_width, half_width)
        flat_users = arrived_users.reshape(total_slots)
        packing = jnp.argsort((flat_users < 0).astype(jnp.int32), stable=True)
        used_slots = jnp.sum((flat_users >= 0).astype(jnp.int32))
        packed_queries = jnp.take(flat_queries, packing, axis=0)
        packed_users = jnp.take(flat_users, packing, axis=0)
        needed = (used_slots + 3) // 4

        def attend_group(group_index, buffer):
            first_slot = group_index * 4
            group_queries = lax.dynamic_slice_in_dim(packed_queries, first_slot, 4, 0)
            group_users = lax.dynamic_slice_in_dim(packed_users, first_slot, 4, 0)
            result = prefix_attention(group_queries, group_users, prefix_keys, prefix_values)
            return lax.dynamic_update_slice_in_dim(buffer, result, first_slot, 0)

        packed_out = lax.fori_loop(
            0, needed, attend_group, jnp.zeros((total_slots, block_width, half_width), jnp.bfloat16)
        )
        inverse = jnp.argsort(packing)
        attended_slots = jnp.take(packed_out, inverse, axis=0)
        return lax.all_to_all(
            attended_slots.reshape(sources, per_source, block_width, half_width),
            "users",
            split_axis=0,
            concat_axis=0,
            tiled=True,
        )

    returned = items_in_groups((outgoing, slot_user), "users", 0, 0, serve_slots, 1, 1)
    prefix_part = jnp.take(returned.reshape(slot_count, block_width * half_width), position, axis=0)
    prefix_part = prefix_part.reshape(row_count, heads_here, HEAD_DIM).astype(jnp.float32)
    query_heads = queries.astype(jnp.float32).reshape(row_count, heads_here, HEAD_DIM)
    self_keys = activated[1].reshape(row_count, heads_here, HEAD_DIM)
    self_values = activated[2].reshape(row_count, heads_here, HEAD_DIM)
    own_term = (
        jax.nn.silu(jnp.sum(query_heads * self_keys, axis=-1) * score_scale)[..., None]
        * self_values
    )
    attended = (prefix_part + own_term).reshape(row_count, half_width)
    totals = lax.psum((jnp.sum(attended, axis=1), jnp.sum(attended * attended, axis=1)), "heads")
    row_mean = totals[0] / HD
    row_var = totals[1] / HD - row_mean * row_mean
    gated = (
        (attended - row_mean[:, None])
        * lax.rsqrt(row_var + EPSILON)[:, None]
        * attn_gain.astype(jnp.float32)
        * activated[3]
    ).astype(jnp.bfloat16)
    partial_out = jnp.dot(
        gated,
        lax.all_gather(w_o, "routers", axis=1, tiled=True),
        preferred_element_type=jnp.float32,
    )
    head_share = sent_and_summed(partial_out, "heads", 1)
    share_cols = head_share.shape[1]
    offset = lax.axis_index("heads") * share_cols
    residual = (
        lax.dynamic_slice_in_dim(flat_items, offset, share_cols, 1).astype(jnp.float32) + head_share
    )
    squares = lax.psum(jnp.sum(residual * residual, axis=1), "heads")
    row_scale = lax.rsqrt(squares / D + EPSILON)
    gain_part = lax.dynamic_slice_in_dim(mlp_gain, offset, share_cols, 0)
    normed = (residual * row_scale[:, None] * gain_part.astype(jnp.float32)).astype(jnp.bfloat16)
    weight_part = lax.dynamic_slice_in_dim(w_one, offset, share_cols, 0)
    inner_sum = taken_together(
        jnp.dot(normed, weight_part, preferred_element_type=jnp.float32), "heads"
    )
    hidden = jax.nn.silu(inner_sum).astype(jnp.bfloat16)
    block_scores = jnp.dot(hidden, w_two, preferred_element_type=jnp.float32).reshape(
        blocks, block_width
    )
    is_valid = lax.broadcasted_iota(jnp.int32, (blocks, block_width), 1) < block_fill[:, None]
    return jnp.where(is_valid, block_scores, jnp.zeros_like(block_scores))


def solution(mesh):
    placed = (
        P(("groups", "users", "routers"), None, None),
        P(("groups", "users", "routers"), None),
        P(("groups", "users", "routers")),
        P(("groups", "users", "routers")),
        P(("groups", "users"), None, "heads"),
        P(("groups", "users"), None, "heads"),
        P(None, "routers", "heads"),
        P("heads"),
        P("heads", "routers"),
        P(),
        P(),
        P(),
    )
    return jax.shard_map(
        local,
        mesh=mesh,
        in_specs=placed,
        out_specs=P(("groups", "users", "routers"), None),
        check_vma=False,
    )
```

profile of v0, /device:TPU:65, one launch (start us, length us, event | category | flops | bytes accessed | tf_op | source)
XLA Modules:
  0.0 428.9 jit_solution(11410321025123503344)
XLA Ops:
  11.2 44.2 %all-to-all-start.3 = ((s32[16,1,1]{2,1,0:T(1,128)}), s32[16,1,1]{2,1,0:T(1,128)S(1)}, u32[]{:S(2)}, u32[]{:S(2)}) async-start(s32[16,1,1]{2,1,0:T(1,128)} %bitcast.11), calls=%async_computation.3 | async-start | bytes 16384 | tf_op jit(solution)/shard_map/all_to_all | solution.py:16
  55.4 55.9 %all-gather.3.cloned.1.call-done = bf16[4,1024,512]{1,2,0:T(8,128)(2,1)} async-done(((bf16[4,128,512]{1,2,0:T(8,128)(2,1)}), bf16[4,1024,512]{1,2,0:T(8,128)(2,1)}) %all-gather.3.cloned.1.call-update) | async-done | bytes 4194320 | tf_op jit(solution)/shard_map/all_gather | solution.py:92
  111.3 7.8 %bitcast_multiply_fusion = f32[4,1024,512]{1,2,0:T(8,128)S(1)} fusion(bf16[4,1024,512]{1,2,0:T(8,128)(2,1)} %all-gather.3.cloned.1.call-done, bf16[1024,1024,1]{1,0,2:T(8,128)(2,1)} %bitcast.171), kind=kOutput, calls=%fused_computation.54 | convolution fusion | flops 4303355904 | bytes 14680064 | tf_op jit(solution)/shard_map/rk,pkc->prc/dot_general | solution.py:89
  119.1 3.2 copy-done.3
  126.9 9.9 %all-to-all-start = ((s32[16,1,1]{2,1,0:T(1,128)}), s32[16,1,1]{2,1,0:T(1,128)S(1)}, u32[]{:S(2)}, u32[]{:S(2)}) async-start(s32[16,1,1]{2,1,0:T(1,128)} %bitcast.6), calls=%async_computation | async-start | bytes 16384 | tf_op jit(solution)/shard_map/all_to_all | solution.py:16
  138.2 9.6 %all-to-all-done = s32[16,1,1]{2,1,0:T(1,128)S(1)} async-done(((s32[16,1,1]{2,1,0:T(1,128)}), s32[16,1,1]{2,1,0:T(1,128)S(1)}, u32[]{:S(2)}, u32[]{:S(2)}) %all-to-all-start) | async-done | bytes 96 | tf_op jit(solution)/shard_map/all_to_all | solution.py:16
  147.8 4.1 all-to-all-start.4
  161.9 35.7 %all-to-all-done.4 = bf16[16,1,64,512]{3,2,1,0:T(8,128)(2,1)S(1)} async-done(((bf16[16,1,64,512]{3,2,1,0:T(8,128)(2,1)}), bf16[16,1,64,512]{3,2,1,0:T(8,128)(2,1)S(1)}, u32[]{:S(2)}, u32[]{:S(2)}) %all-to-all-start.4) | async-done | bytes 1048608 | tf_op jit(solution)/shard_map/all_to_all | solution.py:16
  197.6 10.8 %all-to-all-start.1 = ((bf16[16,1,64,512]{3,2,1,0:T(8,128)(2,1)}), bf16[16,1,64,512]{3,2,1,0:T(8,128)(2,1)}, u32[]{:S(2)}, u32[]{:S(2)}) async-start(bf16[16,1,64,512]{3,2,1,0:T(8,128)(2,1)} %get-tuple-element.142), calls=%async_computation.1 | async-start | bytes 2097152 | tf_op jit(solution)/shard_map/all_to_all | solution.py:16
  215.5 37.3 %all-to-all-done.1 = bf16[16,1,64,512]{3,2,1,0:T(8,128)(2,1)} async-done(((bf16[16,1,64,512]{3,2,1,0:T(8,128)(2,1)}), bf16[16,1,64,512]{3,2,1,0:T(8,128)(2,1)}, u32[]{:S(2)}, u32[]{:S(2)}) %all-to-all-start.1) | async-done | bytes 1048608 | tf_op jit(solution)/shard_map/all_to_all | solution.py:16
  252.8 13.8 %all-to-all-start.5 = ((bf16[16,1,64,512]{3,2,1,0:T(8,128)(2,1)}), bf16[16,1,64,512]{3,2,1,0:T(8,128)(2,1)}, u32[]{:S(2)}, u32[]{:S(2)}) async-start(bf16[16,1,64,512]{3,2,1,0:T(8,128)(2,1)} %select_bitcast_fusion.4), calls=%async_computation.5 | async-start | bytes 2097152 | tf_op jit(solution)/shard_map/all_to_all | solution.py:137
  270.7 24.7 %while.20 = (s32[]{:T(128)}, bf16[16,64,512]{2,1,0:T(8,128)(2,1)}, s32[]{:T(128)}, s32[16]{0:T(128)S(1)}, bf16[2,256,512]{2,1,0:T(8,128)(2,1)S(1)}, /*index=5*/b...) while((s32[]{:T(128)}, bf16[16,64,512]{2,1,0:T(8,128)(2,1)}, ...), condition=%wide.region_5.9_spmd, body=%wide.region_4.8_spmd.sunk | while | flops 136971280 | bytes 11538695 | solution.py:132
  273.0 2.8 select_bitcast_fusion.8
  281.3 2.8 select_bitcast_fusion.8
  289.5 2.8 select_bitcast_fusion.8
  298.4 13.3 %all-to-all-done.5 = bf16[16,1,64,512]{3,2,1,0:T(8,128)(2,1)} async-done(((bf16[16,1,64,512]{3,2,1,0:T(8,128)(2,1)}), bf16[16,1,64,512]{3,2,1,0:T(8,128)(2,1)}, u32[]{:S(2)}, u32[]{:S(2)}) %all-to-all-start.5) | async-done | bytes 1048608 | tf_op jit(solution)/shard_map/all_to_all | solution.py:137
  311.8 13.0 %all-to-all-start.2 = ((bf16[16,1,64,512]{3,2,1,0:T(8,128)(2,1)}), bf16[16,1,64,512]{3,2,1,0:T(8,128)(2,1)}, u32[]{:S(2)}, u32[]{:S(2)}) async-start(bf16[16,1,64,512]{3,2,1,0:T(8,128)(2,1)} %select_bitcast_fusion.5), calls=%async_computation.2 | async-start | bytes 2097152 | tf_op jit(solution)/shard_map/all_to_all | solution.py:137
  325.9 41.3 %all-gather.5.cloned.1.call-done = bf16[512,1024]{1,0:T(8,128)(2,1)} async-done(((bf16[512,128]{1,0:T(8,128)(2,1)}), bf16[512,1024]{1,0:T(8,128)(2,1)}) %all-gather.5.cloned.1.call-update) | async-done | bytes 1048592 | tf_op jit(solution)/shard_map/all_gather | solution.py:167
  383.9 7.8 %all-reduce = (f32[1024]{0:T(1024)S(1)}, f32[1024]{0:T(1024)S(1)}) all-reduce(f32[1024]{0:T(1024)S(1)} %get-tuple-element.95, f32[1024]{0:T(1024)S(1)} %get-tuple-element.94), channel_id=1, replica_groups=mesh['groups'=2,'users'=16,'routers'=8,'heads'=2] {'heads'}, use_global_device_ids=true, to_apply=%region_16.20 | all-reduce | flops 2048 | bytes 16384 | tf_op jit(solution)/shard_map/psum | solution.py:156
  391.8 2.9 fusion.37
  396.0 8.2 %all_to_all.48 = f32[2,1024,512]{2,1,0:T(8,128)} all-to-all(f32[2,1024,512]{2,1,0:T(8,128)S(1)} %convolution_bitcast_fusion), channel_id=1, replica_groups=mesh['groups'=2,'users'=16,'routers'=8,'heads'=2] {'heads'}, dimensions={0} | all-to-all | bytes 8388608 | tf_op jit(solution)/shard_map/all_to_all | solution.py:37
  404.1 2.9 reduce_sum.100
  408.6 2.6 psum.23
  413.0 5.4 %all_to_all.49 = f32[2,1024,256]{2,1,0:T(8,128)S(1)} all-to-all(f32[2,1024,256]{2,1,0:T(8,128)S(1)} %broadcast_in_dim.74), channel_id=1, replica_groups=mesh['groups'=2,'users'=16,'routers'=8,'heads'=2] {'heads'}, dimensions={0} | all-to-all | bytes 4194304 | tf_op jit(solution)/shard_map/all_to_all | solution.py:43
  (129 shorter events, 75.8 us)
Async XLA Ops:
  6.5 404.6 %copy-start = (bf16[1024,256]{1,0:T(8,128)(2,1)S(1)}, bf16[1024,256]{1,0:T(8,128)(2,1)}, u32[]{:S(2)}) copy-start(bf16[1024,256]{1,0:T(8,128)(2,1)} %param.32) | copy-start | bytes 1572868
  6.6 104.8 %all-gather.3.cloned.1.call-start = ((), (), s32[]{:S(2)}) async-start(), calls=%async_computation.8 | async-start | bytes 4718592 | tf_op jit(solution)/shard_map/all_gather | solution.py:92
  11.2 115.7 %all-to-all-start.3 = ((s32[16,1,1]{2,1,0:T(1,128)}), s32[16,1,1]{2,1,0:T(1,128)S(1)}, u32[]{:S(2)}, u32[]{:S(2)}) async-start(s32[16,1,1]{2,1,0:T(1,128)} %bitcast.11), calls=%async_computation.3 | async-start | bytes 16384 | tf_op jit(solution)/shard_map/all_to_all | solution.py:16
  119.1 3.2 copy-start.3
  126.9 20.9 %all-to-all-start = ((s32[16,1,1]{2,1,0:T(1,128)}), s32[16,1,1]{2,1,0:T(1,128)S(1)}, u32[]{:S(2)}, u32[]{:S(2)}) async-start(s32[16,1,1]{2,1,0:T(1,128)} %bitcast.6), calls=%async_computation | async-start | bytes 16384 | tf_op jit(solution)/shard_map/all_to_all | solution.py:16
  147.8 49.8 %all-to-all-start.4 = ((bf16[16,1,64,512]{3,2,1,0:T(8,128)(2,1)}), bf16[16,1,64,512]{3,2,1,0:T(8,128)(2,1)S(1)}, u32[]{:S(2)}, u32[]{:S(2)}) async-start(bf16[16,1,64,512]{3,2,1,0:T(8,128)(2,1)} %get-tuple-element.143), calls=%async_computation.4 | async-start | bytes 2097152 | tf_op jit(solution)/shard_map/all_to_all | solution.py:16
  197.6 10.8 %copy-start.6 = (bf16[16,1,64,512]{3,2,1,0:T(8,128)(2,1)}, bf16[16,1,64,512]{3,2,1,0:T(8,128)(2,1)S(1)}, u32[]{:S(2)}) copy-start(bf16[16,1,64,512]{3,2,1,0:T(8,128)(2,1)S(1)} %all-to-all-done.4) | copy-start | bytes 3145732
  197.6 55.2 %all-to-all-start.1 = ((bf16[16,1,64,512]{3,2,1,0:T(8,128)(2,1)}), bf16[16,1,64,512]{3,2,1,0:T(8,128)(2,1)}, u32[]{:S(2)}, u32[]{:S(2)}) async-start(bf16[16,1,64,512]{3,2,1,0:T(8,128)(2,1)} %get-tuple-element.142), calls=%async_computation.1 | async-start | bytes 2097152 | tf_op jit(solution)/shard_map/all_to_all | solution.py:16
  210.3 2.3 copy-start.1
  210.3 2.2 copy-start.2
  252.8 58.9 %all-to-all-start.5 = ((bf16[16,1,64,512]{3,2,1,0:T(8,128)(2,1)}), bf16[16,1,64,512]{3,2,1,0:T(8,128)(2,1)}, u32[]{:S(2)}, u32[]{:S(2)}) async-start(bf16[16,1,64,512]{3,2,1,0:T(8,128)(2,1)} %select_bitcast_fusion.4), calls=%async_computation.5 | async-start | bytes 2097152 | tf_op jit(solution)/shard_map/all_to_all | solution.py:137
  297.2 28.3 %copy-start.12 = (bf16[256]{0:T(256)(128)(2,1)S(1)}, bf16[256]{0:T(256)(128)(2,1)}, u32[]{:S(2)}) copy-start(bf16[256]{0:T(256)(128)(2,1)} %param.33) | copy-start | bytes 1540
  297.2 28.4 %copy-start.9 = (bf16[512]{0:T(512)(128)(2,1)S(1)}, bf16[512]{0:T(512)(128)(2,1)}, u32[]{:S(2)}) copy-start(bf16[512]{0:T(512)(128)(2,1)} %param.29) | copy-start | bytes 3076
  297.3 28.4 %copy-start.8 = (s32[16,1]{0,1:T(1,128)S(1)}, s32[16,1]{0,1:T(1,128)}, u32[]{:S(2)}) copy-start(s32[16,1]{0,1:T(1,128)} %param.23) | copy-start | bytes 196
  297.3 28.5 %copy-start.10 = (bf16[1024]{0:T(1024)(128)(2,1)S(1)}, bf16[1024]{0:T(1024)(128)(2,1)}, u32[]{:S(2)}) copy-start(bf16[1024]{0:T(1024)(128)(2,1)} %param.31) | copy-start | bytes 6148
  298.4 71.1 %copy-start.5 = (f32[1,1024,512]{1,2,0:T(8,128)S(1)}, f32[1,1024,512]{1,2,0:T(8,128)}, u32[]{:S(2)}) copy-start(f32[1,1024,512]{1,2,0:T(8,128)} %get-tuple-element.136) | copy-start | bytes 6291460
  311.8 58.2 %all-to-all-start.2 = ((bf16[16,1,64,512]{3,2,1,0:T(8,128)(2,1)}), bf16[16,1,64,512]{3,2,1,0:T(8,128)(2,1)}, u32[]{:S(2)}, u32[]{:S(2)}) async-start(bf16[16,1,64,512]{3,2,1,0:T(8,128)(2,1)} %select_bitcast_fusion.5), calls=%async_computation.2 | async-start | bytes 2097152 | tf_op jit(solution)/shard_map/all_to_all | solution.py:137
  324.8 42.4 %all-gather.5.cloned.1.call-start = ((), (), s32[]{:S(2)}) async-start(), calls=%async_computation.9 | async-start | bytes 1179648 | tf_op jit(solution)/shard_map/all_gather | solution.py:167
  375.1 2.5 copy-start.4
  391.8 2.9 copy-start.7
  419.7 1.7 copy-start.11
Sparse Core Ops, SparseCore 0:
  9.4 101.9 all-gather.2
  327.6 39.5 all-gather.4
where the time goes:
time: 431 us; the launch traced here: 429 us
  waiting for transfers between devices  194 us (45%)
  starting transfers between devices  95.8 us (22%)
  local copies, waits for them, and re-layouts  41.8 us (10%)
  other arithmetic  37.5 us (9%)
  blocking collectives  23.9 us (6%)
  matrix products  20.5 us (5%)
  between operations  15.1 us (4%)
    all_to_all x4, waiting for transfers between devices, moved(): lax.all_to_all(group, axis, split_axis=split_dim, concat_axis=concat_dim,...  82.6 us
    all_to_all x4, starting transfers between devices, moved(): lax.all_to_all(group, axis, split_axis=split_dim, concat_axis=concat_dim,...  69 us
    all_gather x1, waiting for transfers between devices, local(): lax.all_gather(w_in, 'routers', axis=1, tiled=True)  55.9 us
    all_gather x1, waiting for transfers between devices, local(): lax.all_gather(w_o, 'routers', axis=1, tiled=True)  41.3 us
    all_to_all x2, starting transfers between devices, serve_slots(): lax.all_to_all(attended_slots.reshape(sources, per_source, block_width, h...  26.7 us
    all_to_all x2, waiting for transfers between devices, serve_slots(): lax.all_to_all(attended_slots.reshape(sources, per_source, block_width, h...  13.6 us
    gather x5, local copies, waits for them, and re-layouts, local(): jnp.take(returned.reshape(slot_count, block_width * half_width), position...  8.96 us
  transfers between devices with their start and end apart: 8, of which 7 were waited for; matrix products, arithmetic and copies ran while one was open for 15% of the time, Pallas kernels for 0%

commit v1 on v0

--- a/solution.py
+++ b/solution.py
@@ -164,7 +164,9 @@
     ).astype(jnp.bfloat16)
     partial_out = jnp.dot(
         gated,
-        lax.all_gather(w_o, "routers", axis=1, tiled=True),
+        jnp.concatenate(
+            lax.all_to_all(jnp.stack([w_o] * lax.axis_size("routers")), "routers", 0, 0), axis=1
+        ),
         preferred_element_type=jnp.float32,
     )
     head_share = sent_and_summed(partial_out, "heads", 1)

time: 431 us -> 442 us (1.026)
    all_to_all x2, waiting for transfers between devices: 13.6 us -> 58.3 us  [serve_slots(): lax.all_to_all(attended_slots.reshape(sources, per_source, block_width, h...]
    all_gather x1 -> x0, waiting for transfers between devices: 41.3 us -> none  [local(): lax.all_gather(w_o, 'routers', axis=1, tiled=True)]
    all_to_all x0 -> x1, starting transfers between devices: none -> 4.42 us  [local(): lax.all_to_all(jnp.stack([w_o] * lax.axis_size('routers')), 'routers', 0, 0)]
  transfers between devices with their start and end apart: 8 -> 8, of which waited for: 7 -> 6; matrix products, arithmetic and copies ran while one was open for 15% -> 18% of each run, Pallas kernels for 0% -> 0%
where the time goes in v1:
time: 442 us; the launch traced here: 440 us
  waiting for transfers between devices  197 us (45%)
  starting transfers between devices  100 us (23%)
  local copies, waits for them, and re-layouts  40.8 us (9%)
  other arithmetic  37.5 us (8%)
  blocking collectives  28 us (6%)
  matrix products  21.7 us (5%)
  between operations  15.1 us (3%)
    all_to_all x4, waiting for transfers between devices, moved(): lax.all_to_all(group, axis, split_axis=split_dim, concat_axis=concat_dim,...  82.6 us
    all_to_all x4, starting transfers between devices, moved(): lax.all_to_all(group, axis, split_axis=split_dim, concat_axis=concat_dim,...  69 us
    all_to_all x2, waiting for transfers between devices, serve_slots(): lax.all_to_all(attended_slots.reshape(sources, per_source, block_width, h...  58.3 us
    all_gather x1, waiting for transfers between devices, local(): lax.all_gather(w_in, 'routers', axis=1, tiled=True)  55.9 us
    all_to_all x2, starting transfers between devices, serve_slots(): lax.all_to_all(attended_slots.reshape(sources, per_source, block_width, h...  26.7 us
    all_to_all x1, blocking collectives, sent_and_summed(): lax.all_to_all(tiles, axis, split_axis=0, concat_axis=0, tiled=True)  12.2 us
    gather x5, local copies, waits for them, and re-layouts, local(): jnp.take(returned.reshape(slot_count, block_width * half_width), position...  8.96 us
  transfers between devices with their start and end apart: 8, of which 6 were waited for; matrix products, arithmetic and copies ran while one was open for 18% of the time, Pallas kernels for 0%

profile of v1, /device:TPU:65, one launch (start us, length us, event | category | flops | bytes accessed | tf_op | source)
XLA Modules:
  0.0 440.2 jit_solution(1906802080212376735)
XLA Ops:
  11.2 44.2 %all-to-all-start.3 = ((s32[16,1,1]{2,1,0:T(1,128)}), s32[16,1,1]{2,1,0:T(1,128)S(1)}, u32[]{:S(2)}, u32[]{:S(2)}) async-start(s32[16,1,1]{2,1,0:T(1,128)} %bitcast.11), calls=%async_computation.3 | async-start | bytes 16384 | tf_op jit(solution)/shard_map/all_to_all | solution.py:16
  55.4 55.9 %all-gather.2.cloned.1.call-done = bf16[4,1024,512]{1,2,0:T(8,128)(2,1)} async-done(((bf16[4,128,512]{1,2,0:T(8,128)(2,1)}), bf16[4,1024,512]{1,2,0:T(8,128)(2,1)}) %all-gather.2.cloned.1.call-update) | async-done | bytes 4194320 | tf_op jit(solution)/shard_map/all_gather | solution.py:92
  111.3 7.8 %bitcast_multiply_fusion = f32[4,1024,512]{1,2,0:T(8,128)S(1)} fusion(bf16[4,1024,512]{1,2,0:T(8,128)(2,1)} %all-gather.2.cloned.1.call-done, bf16[1024,1024,1]{1,0,2:T(8,128)(2,1)} %bitcast.175), kind=kOutput, calls=%fused_computation.54 | convolution fusion | flops 4303355904 | bytes 14680064 | tf_op jit(solution)/shard_map/rk,pkc->prc/dot_general | solution.py:89
  119.1 3.2 copy-done.3
  126.9 9.9 %all-to-all-start = ((s32[16,1,1]{2,1,0:T(1,128)}), s32[16,1,1]{2,1,0:T(1,128)S(1)}, u32[]{:S(2)}, u32[]{:S(2)}) async-start(s32[16,1,1]{2,1,0:T(1,128)} %bitcast.6), calls=%async_computation | async-start | bytes 16384 | tf_op jit(solution)/shard_map/all_to_all | solution.py:16
  138.2 9.6 %all-to-all-done = s32[16,1,1]{2,1,0:T(1,128)S(1)} async-done(((s32[16,1,1]{2,1,0:T(1,128)}), s32[16,1,1]{2,1,0:T(1,128)S(1)}, u32[]{:S(2)}, u32[]{:S(2)}) %all-to-all-start) | async-done | bytes 96 | tf_op jit(solution)/shard_map/all_to_all | solution.py:16
  147.8 4.1 all-to-all-start.4
  161.9 35.7 %all-to-all-done.4 = bf16[16,1,64,512]{3,2,1,0:T(8,128)(2,1)S(1)} async-done(((bf16[16,1,64,512]{3,2,1,0:T(8,128)(2,1)}), bf16[16,1,64,512]{3,2,1,0:T(8,128)(2,1)S(1)}, u32[]{:S(2)}, u32[]{:S(2)}) %all-to-all-start.4) | async-done | bytes 1048608 | tf_op jit(solution)/shard_map/all_to_all | solution.py:16
  197.6 10.8 %all-to-all-start.1 = ((bf16[16,1,64,512]{3,2,1,0:T(8,128)(2,1)}), bf16[16,1,64,512]{3,2,1,0:T(8,128)(2,1)}, u32[]{:S(2)}, u32[]{:S(2)}) async-start(bf16[16,1,64,512]{3,2,1,0:T(8,128)(2,1)} %get-tuple-element.142), calls=%async_computation.1 | async-start | bytes 2097152 | tf_op jit(solution)/shard_map/all_to_all | solution.py:16
  215.5 37.3 %all-to-all-done.1 = bf16[16,1,64,512]{3,2,1,0:T(8,128)(2,1)} async-done(((bf16[16,1,64,512]{3,2,1,0:T(8,128)(2,1)}), bf16[16,1,64,512]{3,2,1,0:T(8,128)(2,1)}, u32[]{:S(2)}, u32[]{:S(2)}) %all-to-all-start.1) | async-done | bytes 1048608 | tf_op jit(solution)/shard_map/all_to_all | solution.py:16
  252.8 13.8 %all-to-all-start.5 = ((bf16[16,1,64,512]{3,2,1,0:T(8,128)(2,1)}), bf16[16,1,64,512]{3,2,1,0:T(8,128)(2,1)}, u32[]{:S(2)}, u32[]{:S(2)}) async-start(bf16[16,1,64,512]{3,2,1,0:T(8,128)(2,1)} %select_bitcast_fusion.4), calls=%async_computation.5 | async-start | bytes 2097152 | tf_op jit(solution)/shard_map/all_to_all | solution.py:137
  270.7 24.7 %while.20 = (s32[]{:T(128)}, bf16[16,64,512]{2,1,0:T(8,128)(2,1)}, s32[]{:T(128)}, s32[16]{0:T(128)S(1)}, bf16[2,256,512]{2,1,0:T(8,128)(2,1)S(1)}, /*index=5*/b...) while((s32[]{:T(128)}, bf16[16,64,512]{2,1,0:T(8,128)(2,1)}, ...), condition=%wide.region_5.9_spmd, body=%wide.region_4.8_spmd.sunk | while | flops 136971280 | bytes 11538695 | solution.py:132
  273.0 2.8 select_bitcast_fusion.8
  281.3 2.8 select_bitcast_fusion.8
  289.5 2.8 select_bitcast_fusion.8
  298.5 13.3 %all-to-all-done.5 = bf16[16,1,64,512]{3,2,1,0:T(8,128)(2,1)} async-done(((bf16[16,1,64,512]{3,2,1,0:T(8,128)(2,1)}), bf16[16,1,64,512]{3,2,1,0:T(8,128)(2,1)}, u32[]{:S(2)}, u32[]{:S(2)}) %all-to-all-start.5) | async-done | bytes 1048608 | tf_op jit(solution)/shard_map/all_to_all | solution.py:137
  311.8 13.0 %all-to-all-start.2 = ((bf16[16,1,64,512]{3,2,1,0:T(8,128)(2,1)}), bf16[16,1,64,512]{3,2,1,0:T(8,128)(2,1)}, u32[]{:S(2)}, u32[]{:S(2)}) async-start(bf16[16,1,64,512]{3,2,1,0:T(8,128)(2,1)} %select_bitcast_fusion.5), calls=%async_computation.2 | async-start | bytes 2097152 | tf_op jit(solution)/shard_map/all_to_all | solution.py:137
  324.9 45.0 %all-to-all-done.2 = bf16[16,1,64,512]{3,2,1,0:T(8,128)(2,1)} async-done(((bf16[16,1,64,512]{3,2,1,0:T(8,128)(2,1)}), bf16[16,1,64,512]{3,2,1,0:T(8,128)(2,1)}, u32[]{:S(2)}, u32[]{:S(2)}) %all-to-all-start.2) | async-done | bytes 1048608 | tf_op jit(solution)/shard_map/all_to_all | solution.py:137
  371.1 4.4 %all-to-all-start.6 = ((bf16[8,512,128]{1,2,0:T(8,128)(2,1)}), bf16[8,512,128]{1,2,0:T(8,128)(2,1)}, u32[]{:S(2)}, u32[]{:S(2)}) async-start(bf16[8,512,128]{1,2,0:T(8,128)(2,1)} %stack.2), calls=%async_computation.6 | async-start | bytes 2097152 | tf_op jit(solution)/shard_map/all_to_all | solution.py:168
  390.0 7.8 %all-reduce = (f32[1024]{0:T(1024)S(1)}, f32[1024]{0:T(1024)S(1)}) all-reduce(f32[1024]{0:T(1024)S(1)} %get-tuple-element.95, f32[1024]{0:T(1024)S(1)} %get-tuple-element.94), channel_id=1, replica_groups=mesh['groups'=2,'users'=16,'routers'=8,'heads'=2] {'heads'}, use_global_device_ids=true, to_apply=%region_16.20 | all-reduce | flops 2048 | bytes 16384 | tf_op jit(solution)/shard_map/psum | solution.py:156
  397.8 2.8 fusion.37
  403.2 12.2 %all_to_all.53 = f32[2,1024,512]{2,1,0:T(8,128)} all-to-all(f32[2,1024,512]{2,1,0:T(8,128)S(1)} %convolution_bitcast_fusion), channel_id=1, replica_groups=mesh['groups'=2,'users'=16,'routers'=8,'heads'=2] {'heads'}, dimensions={0} | all-to-all | bytes 8388608 | tf_op jit(solution)/shard_map/all_to_all | solution.py:37
  415.4 2.9 reduce_sum.100
  424.3 5.4 %all_to_all.54 = f32[2,1024,256]{2,1,0:T(8,128)S(1)} all-to-all(f32[2,1024,256]{2,1,0:T(8,128)S(1)} %broadcast_in_dim.74), channel_id=1, replica_groups=mesh['groups'=2,'users'=16,'routers'=8,'heads'=2] {'heads'}, dimensions={0} | all-to-all | bytes 4194304 | tf_op jit(solution)/shard_map/all_to_all | solution.py:43
  (129 shorter events, 77.5 us)
Async XLA Ops:
  6.5 415.9 %copy-start = (bf16[1024,256]{1,0:T(8,128)(2,1)S(1)}, bf16[1024,256]{1,0:T(8,128)(2,1)}, u32[]{:S(2)}) copy-start(bf16[1024,256]{1,0:T(8,128)(2,1)} %param.32) | copy-start | bytes 1572868
  6.6 104.8 %all-gather.2.cloned.1.call-start = ((), (), s32[]{:S(2)}) async-start(), calls=%async_computation.9 | async-start | bytes 4718592 | tf_op jit(solution)/shard_map/all_gather | solution.py:92
  11.2 115.7 %all-to-all-start.3 = ((s32[16,1,1]{2,1,0:T(1,128)}), s32[16,1,1]{2,1,0:T(1,128)S(1)}, u32[]{:S(2)}, u32[]{:S(2)}) async-start(s32[16,1,1]{2,1,0:T(1,128)} %bitcast.11), calls=%async_computation.3 | async-start | bytes 16384 | tf_op jit(solution)/shard_map/all_to_all | solution.py:16
  119.1 3.2 copy-start.3
  126.9 20.9 %all-to-all-start = ((s32[16,1,1]{2,1,0:T(1,128)}), s32[16,1,1]{2,1,0:T(1,128)S(1)}, u32[]{:S(2)}, u32[]{:S(2)}) async-start(s32[16,1,1]{2,1,0:T(1,128)} %bitcast.6), calls=%async_computation | async-start | bytes 16384 | tf_op jit(solution)/shard_map/all_to_all | solution.py:16
  147.8 49.8 %all-to-all-start.4 = ((bf16[16,1,64,512]{3,2,1,0:T(8,128)(2,1)}), bf16[16,1,64,512]{3,2,1,0:T(8,128)(2,1)S(1)}, u32[]{:S(2)}, u32[]{:S(2)}) async-start(bf16[16,1,64,512]{3,2,1,0:T(8,128)(2,1)} %get-tuple-element.143), calls=%async_computation.4 | async-start | bytes 2097152 | tf_op jit(solution)/shard_map/all_to_all | solution.py:16
  197.6 10.8 %copy-start.6 = (bf16[16,1,64,512]{3,2,1,0:T(8,128)(2,1)}, bf16[16,1,64,512]{3,2,1,0:T(8,128)(2,1)S(1)}, u32[]{:S(2)}) copy-start(bf16[16,1,64,512]{3,2,1,0:T(8,128)(2,1)S(1)} %all-to-all-done.4) | copy-start | bytes 3145732
  197.6 55.2 %all-to-all-start.1 = ((bf16[16,1,64,512]{3,2,1,0:T(8,128)(2,1)}), bf16[16,1,64,512]{3,2,1,0:T(8,128)(2,1)}, u32[]{:S(2)}, u32[]{:S(2)}) async-start(bf16[16,1,64,512]{3,2,1,0:T(8,128)(2,1)} %get-tuple-element.142), calls=%async_computation.1 | async-start | bytes 2097152 | tf_op jit(solution)/shard_map/all_to_all | solution.py:16
  210.3 2.3 copy-start.1
  210.3 2.2 copy-start.2
  252.8 58.9 %all-to-all-start.5 = ((bf16[16,1,64,512]{3,2,1,0:T(8,128)(2,1)}), bf16[16,1,64,512]{3,2,1,0:T(8,128)(2,1)}, u32[]{:S(2)}, u32[]{:S(2)}) async-start(bf16[16,1,64,512]{3,2,1,0:T(8,128)(2,1)} %select_bitcast_fusion.4), calls=%async_computation.5 | async-start | bytes 2097152 | tf_op jit(solution)/shard_map/all_to_all | solution.py:137
  297.2 27.5 %copy-start.7 = (bf16[512,128]{1,0:T(8,128)(2,1)S(1)}, bf16[512,128]{1,0:T(8,128)(2,1)}, u32[]{:S(2)}) copy-start(bf16[512,128]{1,0:T(8,128)(2,1)} %param.30) | copy-start | bytes 393220
  311.8 58.2 %all-to-all-start.2 = ((bf16[16,1,64,512]{3,2,1,0:T(8,128)(2,1)}), bf16[16,1,64,512]{3,2,1,0:T(8,128)(2,1)}, u32[]{:S(2)}, u32[]{:S(2)}) async-start(bf16[16,1,64,512]{3,2,1,0:T(8,128)(2,1)} %select_bitcast_fusion.5), calls=%async_computation.2 | async-start | bytes 2097152 | tf_op jit(solution)/shard_map/all_to_all | solution.py:137
  324.8 50.7 %copy-start.12 = (bf16[256]{0:T(256)(128)(2,1)S(1)}, bf16[256]{0:T(256)(128)(2,1)}, u32[]{:S(2)}) copy-start(bf16[256]{0:T(256)(128)(2,1)} %param.33) | copy-start | bytes 1540
  324.8 50.8 %copy-start.9 = (bf16[512]{0:T(512)(128)(2,1)S(1)}, bf16[512]{0:T(512)(128)(2,1)}, u32[]{:S(2)}) copy-start(bf16[512]{0:T(512)(128)(2,1)} %param.29) | copy-start | bytes 3076
  324.8 50.8 %copy-start.8 = (s32[16,1]{0,1:T(1,128)S(1)}, s32[16,1]{0,1:T(1,128)}, u32[]{:S(2)}) copy-start(s32[16,1]{0,1:T(1,128)} %param.23) | copy-start | bytes 196
  324.8 50.9 %copy-start.10 = (bf16[1024]{0:T(1024)(128)(2,1)S(1)}, bf16[1024]{0:T(1024)(128)(2,1)}, u32[]{:S(2)}) copy-start(bf16[1024]{0:T(1024)(128)(2,1)} %param.31) | copy-start | bytes 6148
  324.8 51.0 %copy-start.5 = (f32[1,1024,512]{1,2,0:T(8,128)S(1)}, f32[1,1024,512]{1,2,0:T(8,128)}, u32[]{:S(2)}) copy-start(f32[1,1024,512]{1,2,0:T(8,128)} %get-tuple-element.136) | copy-start | bytes 6291460
  371.1 29.6 %all-to-all-start.6 = ((bf16[8,512,128]{1,2,0:T(8,128)(2,1)}), bf16[8,512,128]{1,2,0:T(8,128)(2,1)}, u32[]{:S(2)}, u32[]{:S(2)}) async-start(bf16[8,512,128]{1,2,0:T(8,128)(2,1)} %stack.2), calls=%async_computation.6 | async-start | bytes 2097152 | tf_op jit(solution)/shard_map/all_to_all | solution.py:168
  381.2 2.5 copy-start.4
  431.0 1.7 copy-start.11
Sparse Core Ops, SparseCore 0:
  9.4 101.9 all-gather.1
